TPU v7x, 256 devices: a whole 4x4x8 slice. The times are simulated.
256 devices in a mesh: section: 16 (over z, y_hi), seq: 16 (over y_lo, x, core).
Axes of the slice: x: 4, y: 4 (y_hi: 2, y_lo: 2; y = y_hi * 2 + y_lo), z: 8, core: 2. Of those that a mesh axis runs over, the one named last changes fastest.
Arguments:
- queries: bfloat16 [14336, 4096], P(('section', 'seq')), may hold values from -200 to 200
- key_vectors: bfloat16 [14336, 4096], P(('section', 'seq')), may hold values from -6 to 6
- value_vectors: bfloat16 [14336, 4096], P(('section', 'seq')), may hold values from -6 to 6
- noise_levels: int32 [16], replicated, may hold values from 0 to 15
- visible: int32 [16, 16], replicated, may hold values 0 or 1
- level_gates: float32 [16, 4096], replicated, may hold values from 0.5 to 2
Outputs:
- attended: bfloat16 [14336, 4096], P(('section', 'seq'))
All inputs are finite; a program needn't handle non-finite values.
Results may differ from a plain program's by a relative error of at most 0.0045.
Values may be sent and summed in bfloat16 or wider, within the bound.
No kernel may reach another device: no remote copies, remote signals or barrier semaphores. Data moves between devices by JAX's collectives and lax.ppermute only.
A program may use at most 128 MiB of HBM per device.

v0:
```python
import functools
import math

import jax
import jax.numpy as jnp
from jax import lax
from jax.experimental import pallas as pl
from jax.experimental.pallas import tpu as pltpu
from jax.sharding import Mesh
from jax.sharding import PartitionSpec as P


HEAD_DIM = 128
AXES = ("z", "yh", "yl", "x", "core")
HEAD_AXES = ("z", "yh", "yl")
NEGATIVE = -1e30
UNROLL = 4
TO_EXP2 = math.log2(math.e) / math.sqrt(HEAD_DIM)


def attend(sources, first, last, groups, lists, noise, q_ref, *refs):
    refs = list(refs)
    keys, values = [], []
    for kind in sources:
        if kind == "pair":
            ref = refs.pop(0)
            keys.append(ref.at[0])
            values.append(ref.at[1])
        else:
            keys.append(refs.pop(0))
            values.append(refs.pop(0))
    if not first:
        old_m, old_l, old_acc = refs[:3]
        refs = refs[3:]
    if last:
        gate_ref, o_ref, m_ref, l_ref, acc_ref, turned_ref, padded_ref, *scores_ref, done = refs
    else:
        m_ref, l_ref, acc_out, acc_ref, turned_ref, padded_ref, *scores_ref, done = refs
    if first:
        m_ref[...] = jnp.full_like(m_ref, NEGATIVE)
        l_ref[...] = jnp.zeros_like(l_ref)
        acc_ref[...] = jnp.zeros_like(acc_ref)
    else:
        m_ref[...] = old_m[...]
        l_ref[...] = old_l[...]
        fetch = pltpu.make_async_copy(old_acc, acc_ref, done)
        fetch.start()

    pad = HEAD_DIM - q_ref.shape[1]

    def prepare(c, carry):
        turned_ref[c] = jnp.concatenate([v[c] for v in values], axis=0).T
        padded_ref[c] = jnp.concatenate([q_ref[c], jnp.zeros((pad, HEAD_DIM), q_ref.dtype)], axis=0)
        return carry

    lax.fori_loop(0, groups, prepare, 0, unroll=4)

    def scores(i, score_ref):
        block = jnp.concatenate([k[lists[2, i]] for k in keys], axis=0)
        query = jnp.concatenate([padded_ref[lists[0, i]], padded_ref[lists[1, i]]], axis=0)
        score_ref[...] = lax.dot_general(
            block, query, (((1,), (1,)), ((), ())), preferred_element_type=jnp.float32
        )

    def weigh(i, u):
        score = scores_ref[u]
        high = jnp.max(score[...], axis=0, keepdims=True)
        weight = jnp.exp2((score[...] - high) * TO_EXP2)
        total = jnp.sum(weight, axis=0, keepdims=True)
        update = jnp.dot(
            turned_ref[lists[2, i]], weight.astype(jnp.bfloat16), preferred_element_type=jnp.float32
        )
        return high, total, update

    def merge(i, found):
        high, total, update = found
        for part in range(2):
            slot = lists[3 + part, i]
            lanes = slice(part * HEAD_DIM, (part + 1) * HEAD_DIM)
            old = m_ref[slot]
            new = jnp.maximum(old, high[:, lanes])
            keep = jnp.exp2((old - new) * TO_EXP2)
            take = jnp.exp2((high[:, lanes] - new) * TO_EXP2)
            m_ref[slot] = new
            l_ref[slot] = l_ref[slot] * keep + total[:, lanes] * take
            acc_ref[slot] = acc_ref[slot] * keep + update[:, lanes] * take

    for u in range(UNROLL):
        scores(u, scores_ref[u])

    def step(j, carry):
        found = []
        for u in range(UNROLL):
            found.append(weigh(UNROLL * j + u, u))
            scores(UNROLL * (j + 1) + u, scores_ref[u])
        for u in range(UNROLL):
            merge(UNROLL * j + u, found[u])
        return carry

    if not first:
        fetch.wait()

    lax.fori_loop(0, lists[5, 0], step, 0)

    if not last:
        store = pltpu.make_async_copy(acc_ref, acc_out, done)
        store.start()
        store.wait()

    if last:

        def finish(c, carry):
            gate = gate_ref[pl.ds(noise[c], 1), :]
            ratio = (acc_ref[c] / l_ref[c]).T[: q_ref.shape[1]]
            o_ref[c] = (ratio * gate).astype(o_ref.dtype)
            return carry

        lax.fori_loop(0, groups, finish, 0, unroll=4)


def attend_call(sources, first, last, lists, noise, query, operands):
    groups, rows, _ = query.shape
    width = len(sources) * rows
    blocks = groups * (groups + 1) // 2
    vmem = pl.BlockSpec(memory_space=pltpu.VMEM)
    smem = pl.BlockSpec(memory_space=pltpu.SMEM)
    state = [(groups + 1, 1, HEAD_DIM), (groups + 1, 1, HEAD_DIM), (groups + 1, HEAD_DIM, HEAD_DIM)]
    work = [
        pltpu.VMEM((groups, HEAD_DIM, width), jnp.bfloat16),
        pltpu.VMEM((groups, HEAD_DIM, HEAD_DIM), jnp.bfloat16),
    ] + [pltpu.VMEM((width, 2 * HEAD_DIM), jnp.float32)] * UNROLL
    if last:
        out_shape = jax.ShapeDtypeStruct(query.shape, jnp.bfloat16)
        scratch = [pltpu.VMEM(shape, jnp.float32) for shape in state] + work
        out_specs = vmem
    else:
        out_shape = [jax.ShapeDtypeStruct(shape, jnp.float32) for shape in state]
        scratch = [pltpu.VMEM(state[2], jnp.float32)] + work
        out_specs = [vmem, vmem, pl.BlockSpec(memory_space=pltpu.HBM)]
    in_specs = [smem, smem] + [vmem] * (1 + len(operands))
    if not first:
        in_specs[-2 if last else -1] = pl.BlockSpec(memory_space=pltpu.HBM)
    return pl.pallas_call(
        functools.partial(attend, sources, first, last, groups),
        out_shape=out_shape,
        in_specs=in_specs,
        out_specs=out_specs,
        scratch_shapes=scratch + [pltpu.SemaphoreType.DMA],
        compiler_params=pltpu.CompilerParams(vmem_limit_bytes=16 * 1024 * 1024),
        cost_estimate=pl.CostEstimate(
            flops=12 * blocks * rows * width * HEAD_DIM,
            bytes_accessed=4 * len(sources) * query.size,
            transcendentals=blocks * rows * width,
        ),
        name="attend_last" if last else "attend_first",
    )(lists, noise, query, *operands)


def live_pairs(visible):
    groups = visible.shape[0]
    ids = jnp.arange(groups, dtype=jnp.int32)
    c, e = ids[:, None], ids[None, :]
    live = (c == e) | (e < c) & (visible == 1)
    rank = jnp.sum((live[None, :, :] & (ids[None, :] < ids[:, None])[:, :, None]).astype(jnp.int32), axis=1)
    seen = jnp.sum(live.astype(jnp.int32), axis=0)
    pairs = (seen + 1) // 2
    start = jnp.sum(jnp.where(ids[None, :] < ids[:, None], pairs[None, :], 0), axis=1)
    total = jnp.sum(pairs)
    length = sum((n + 1) // 2 for n in range(1, groups + 1)) + 2 * UNROLL - 1
    places = jnp.arange(length, dtype=jnp.int32)
    column = start[None, :] + rank // 2
    rows = []
    for part in range(2):
        here = live & (rank % 2 == part)
        taken = here[None, :, :] & (column[None, :, :] == places[:, None, None])
        found = jnp.any(taken, axis=(1, 2))
        query = jnp.sum(jnp.where(taken, ids[None, :, None], 0), axis=(1, 2))
        key = jnp.sum(jnp.where(taken, ids[None, None, :], 0), axis=(1, 2))
        rows.append((query, key, jnp.where(found, query, groups)))
    (q0, key, s0), (q1, _, s1) = rows
    steps = jnp.broadcast_to((total + UNROLL - 1) // UNROLL, places.shape)
    return jnp.stack([q0, q1, key, s0, s1, steps])


def to_heads(value):
    return value.reshape(value.shape[0], -1, HEAD_DIM).transpose(1, 0, 2)


def pack(k_ref, v_ref, o_ref):
    for h in range(o_ref.shape[0]):
        lanes = slice(h * HEAD_DIM, (h + 1) * HEAD_DIM)
        o_ref[h, 0] = k_ref[:, lanes]
        o_ref[h, 1] = v_ref[:, lanes]


def packed(keys, values):
    tokens, width = keys.shape
    vmem = pl.BlockSpec(memory_space=pltpu.VMEM)
    return pl.pallas_call(
        pack,
        out_shape=jax.ShapeDtypeStruct((width // HEAD_DIM, 2, tokens, HEAD_DIM), keys.dtype),
        in_specs=[vmem, vmem],
        out_specs=vmem,
        compiler_params=pltpu.CompilerParams(vmem_limit_bytes=8 * 1024 * 1024),
        name="pack",
    )(keys, values)


def swapped(value):
    return lax.ppermute(value, "core", [(0, 1), (1, 0)])


def shifted(value, shift):
    size = lax.axis_size("x")
    return lax.ppermute(value, "x", [(i, (i + shift) % size) for i in range(size)])


def exchanged(blocks):
    return lax.all_to_all(blocks, HEAD_AXES, 0, 0, tiled=True)


def attention(queries, key_vectors, value_vectors, noise_levels, visible, level_gates):
    groups = visible.shape[0]
    pair = exchanged(packed(key_vectors, value_vectors))
    key = pair[:, 0].reshape(groups, -1, HEAD_DIM)
    value = pair[:, 1].reshape(groups, -1, HEAD_DIM)
    query = exchanged(to_heads(queries)).reshape(groups, -1, HEAD_DIM)
    key_up, key_down = shifted(key, 1), shifted(key, -1)
    value_up, value_down = shifted(value, 1), shifted(value, -1)
    key_far, value_far = shifted(key_up, 1), shifted(value_down, -1)
    lists = live_pairs(visible)
    head = lax.axis_index(HEAD_AXES)
    gates = lax.dynamic_slice_in_dim(level_gates, head * HEAD_DIM, HEAD_DIM, axis=1)
    early = [key, value, key_up, value_up]
    early = early + [swapped(piece) for piece in early]
    late = [key_down, value_down]
    late = late + [swapped(piece) for piece in late]
    state = attend_call(["two"] * 4, True, False, lists, noise_levels, query, early)
    key_far, value_far, top = lax.optimization_barrier((key_far, value_far, state[0]))
    late = late + [key_far, value_far, swapped(key_far), swapped(value_far), top, *state[1:], gates]
    out = attend_call(["two"] * 4, False, True, lists, noise_levels, query, late)
    back = out.reshape(lax.axis_size(HEAD_AXES), -1, HEAD_DIM)
    back = lax.all_to_all(back, HEAD_AXES, 0, 0, tiled=True)
    return back.transpose(1, 0, 2).reshape(queries.shape)


def solution(mesh):
    split = Mesh(mesh.devices.reshape(8, 2, 2, 4, 2), AXES)
    rows = P(AXES, None)
    return jax.shard_map(
        attention,
        mesh=split,
        in_specs=(rows, rows, rows, P(), P(), P()),
        out_specs=rows,
        check_vma=False,
    )
```

profile of v0, /device:TPU:1, one launch (start us, length us, event | category | flops | bytes accessed | tf_op | source)
XLA Modules:
  0.0 130.5 jit_solution(8925457101549299807)
XLA Ops:
  0.0 1.1 copy-done.1
  1.1 1.0 copy-done.2
  2.1 1.1 pack.1
  3.2 12.2 %all-to-all-start.1 = ((bf16[32,2,56,128]{3,2,1,0:T(8,128)(2,1)}), bf16[32,2,56,128]{3,2,1,0:T(8,128)(2,1)S(1)}, u32[]{:S(2)}, u32[]{:S(2)}) async-start(bf16[32,2,56,128]{3,2,1,0:T(8,128)(2,1)} %pack.1), calls=%async_computation.1 | async-start | bytes 1835008 | tf_op jit(solution)/shard_map/all_to_all | solution.py:219
  16.3 0.8 bitcast_bitcast_fusion
  17.1 21.9 %all-to-all-done.1 = bf16[32,2,56,128]{3,2,1,0:T(8,128)(2,1)S(1)} async-done(((bf16[32,2,56,128]{3,2,1,0:T(8,128)(2,1)}), bf16[32,2,56,128]{3,2,1,0:T(8,128)(2,1)S(1)}, u32[]{:S(2)}, u32[]{:S(2)}) %all-to-all-start.1) | async-done | bytes 917536 | tf_op jit(solution)/shard_map/all_to_all | solution.py:219
  39.0 6.0 %all-to-all-start = ((bf16[32,56,128]{2,1,0:T(8,128)(2,1)}), bf16[32,56,128]{2,1,0:T(8,128)(2,1)S(1)}, u32[]{:S(2)}, u32[]{:S(2)}) async-start(bf16[32,56,128]{2,1,0:T(8,128)(2,1)} %bitcast_bitcast_fusion), calls=%async_computation | async-start | bytes 917504 | tf_op jit(solution)/shard_map/all_to_all | solution.py:219
  45.1 1.3 collective-permute-start.4
  46.4 2.5 %collective-permute-start.8 = (bf16[16,112,128]{2,1,0:T(8,128)(2,1)S(1)}, bf16[16,112,128]{2,1,0:T(8,128)(2,1)}, u32[]{:S(2)}, u32[]{:S(2)}) collective-permute-start(bf16[16,112,128]{2,1,0:T(8,128)(2,1)S(1)} %bitcast.31), channel_id=1, source_target_pairs={{0,1},{1,0},{2,3},{3,2},{4,5},{5,4},{6,7},{7,6},{8,9},{9,8},{10,11... | collective-permute-start | bytes 1376264 | tf_op jit(solution)/shard_map/ppermute | solution.py:210
  48.8 1.2 collective-permute-start.7
  51.3 1.5 %collective-permute-start.1 = (bf16[16,112,128]{2,1,0:T(8,128)(2,1)S(1)}, bf16[16,112,128]{2,1,0:T(8,128)(2,1)S(1)}, u32[]{:S(2)}, u32[]{:S(2)}) collective-permute-start(bf16[16,112,128]{2,1,0:T(8,128)(2,1)S(1)} %bitcast.28), channel_id=1, source_target_pairs={{0,6},{2,0},{4,2},{6,4},{1,7},{3,1},{5,3},{7,5},{8,14},{10,8},{12,... | collective-permute-start | bytes 1376264 | tf_op jit(solution)/shard_map/ppermute | solution.py:215
  52.7 3.5 %collective-permute-done.4.refs_2_ = bf16[16,112,128]{2,1,0:T(8,128)(2,1)S(1)} collective-permute-done((bf16[16,112,128]{2,1,0:T(8,128)(2,1)S(1)}, bf16[16,112,128]{2,1,0:T(8,128)(2,1)S(1)}, u32[]{:S(2)}, u32[]{:S(2)}) %collective-permute-start.4) | collective-permute-done | bytes 458784 | tf_op jit(solution)/shard_map/ppermute | solution.py:215
  56.2 1.3 collective-permute-start
  57.5 8.7 %collective-permute-done.7.refs_3_ = bf16[16,112,128]{2,1,0:T(8,128)(2,1)} collective-permute-done((bf16[16,112,128]{2,1,0:T(8,128)(2,1)S(1)}, bf16[16,112,128]{2,1,0:T(8,128)(2,1)}, u32[]{:S(2)}, u32[]{:S(2)}) %collective-permute-start.7) | collective-permute-done | bytes 458784 | tf_op jit(solution)/shard_map/ppermute | solution.py:215
  66.2 3.0 %collective-permute-start.10 = (bf16[16,112,128]{2,1,0:T(8,128)(2,1)S(1)}, bf16[16,112,128]{2,1,0:T(8,128)(2,1)}, u32[]{:S(2)}, u32[]{:S(2)}) collective-permute-start(bf16[16,112,128]{2,1,0:T(8,128)(2,1)S(1)} %collective-permute-done.4.refs_2_), channel_id=1, source_target_pairs={{0,1},{1,0},{2,3},{3,2},{4,5},{5,4},{6,7},{7,6},{8,9},{9,8},{10,11... | collective-permute-start | bytes 1376264 | tf_op jit(solution)/shard_map/ppermute | solution.py:210
  69.8 2.7 %collective-permute-start.6 = (bf16[16,112,128]{2,1,0:T(8,128)(2,1)S(1)}, bf16[16,112,128]{2,1,0:T(8,128)(2,1)}, u32[]{:S(2)}, u32[]{:S(2)}) collective-permute-start(bf16[16,112,128]{2,1,0:T(8,128)(2,1)S(1)} %collective-permute-done.1.refs_1_), channel_id=1, source_target_pairs={{0,6},{2,0},{4,2},{6,4},{1,7},{3,1},{5,3},{7,5},{8,14},{10,8},{12,... | collective-permute-start | bytes 1376264 | tf_op jit(solution)/shard_map/ppermute | solution.py:215
  72.4 2.7 %collective-permute-start.3 = (bf16[16,112,128]{2,1,0:T(8,128)(2,1)S(1)}, bf16[16,112,128]{2,1,0:T(8,128)(2,1)}, u32[]{:S(2)}, u32[]{:S(2)}) collective-permute-start(bf16[16,112,128]{2,1,0:T(8,128)(2,1)S(1)} %collective-permute-done.1.refs_1_), channel_id=1, source_target_pairs={{0,1},{1,0},{2,3},{3,2},{4,5},{5,4},{6,7},{7,6},{8,9},{9,8},{10,11... | collective-permute-start | bytes 1376264 | tf_op jit(solution)/shard_map/ppermute | solution.py:210
  75.2 12.1 %attend_first.1 = (f32[17,1,128]{2,1,0:T(1,128)S(1)}, f32[17,1,128]{2,1,0:T(1,128)S(1)}, f32[17,128,128]{2,1,0:T(8,128)S(1)}) custom-call(s32[6,79]{1,0:T(8,128)S(1)} %stack.17.lists, s32[16]{0:T(128)S(1)} %copy-done.3, bf16[16,112,128]{2,1,0:T(8,128)(2,1)S(1)} %bitcast.34, bf16[16,112,128]{2,1,0:T(8,128)(2,1)S(1)} %bitcast.33, ...), custom_call_target="tpu_custom_call" | custom-call | flops 10481565696 | bytes 3670016 | tf_op jit(solution)/shard_map/attend_first/pallas_call | solution.py:143
  87.2 1.0 copy-done.4
  89.5 0.9 collective-permute-done.12.refs_6_
  91.0 1.2 copy-done.5
  92.3 12.4 %attend_last.1 = bf16[16,112,128]{2,1,0:T(8,128)(2,1)S(1)} custom-call(s32[6,79]{1,0:T(8,128)S(1)} %stack.17.lists, s32[16]{0:T(128)S(1)} %copy-done.3, bf16[16,112,128]{2,1,0:T(8,128)(2,1)S(1)} %bitcast.35, bf16[16,112,128]{2,1,0:T(8,128)(2,1)S(1)} %collective-permute-done.refs_0_, bf16[16,112,128]{2,1,0:T(8,128)(2,1)S(1)} %collective-permute-done.1.refs_1_, ...), custom_call_target="tpu_custom_call" | custom-call | flops 10481565696 | bytes 3670016 | tf_op jit(solution)/shard_map/attend_last/pallas_call | solution.py:143
  104.7 25.0 %all_to_all.15 = bf16[32,56,128]{2,1,0:T(8,128)(2,1)S(1)} all-to-all(bf16[32,56,128]{2,1,0:T(8,128)(2,1)S(1)} %bitcast.36), channel_id=1, replica_groups=mesh['z'=8,'yh'=2,'yl'=2,'x'=4,'core'=2] {'z','yh','yl'}, dimensions={0} | all-to-all | bytes 917504 | tf_op jit(solution)/shard_map/all_to_all | solution.py:243
  129.7 0.8 copy_bitcast_fusion
  (42 shorter events, 3.9 us)
Async XLA Ops:
  0.0 16.3 %copy-start = (bf16[56,4096]{1,0:T(8,128)(2,1)S(1)}, bf16[56,4096]{1,0:T(8,128)(2,1)}, u32[]{:S(2)}) copy-start(bf16[56,4096]{1,0:T(8,128)(2,1)} %param.6) | copy-start | bytes 1376260
  0.0 1.1 copy-start.1
  1.1 1.0 copy-start.2
  3.2 12.2 %copy-start.6 = (s32[16,16]{1,0:T(8,128)S(1)}, s32[16,16]{1,0:T(8,128)}, u32[]{:S(2)}) copy-start(s32[16,16]{1,0:T(8,128)} %param.10) | copy-start | bytes 3076
  3.2 35.8 %all-to-all-start.1 = ((bf16[32,2,56,128]{3,2,1,0:T(8,128)(2,1)}), bf16[32,2,56,128]{3,2,1,0:T(8,128)(2,1)S(1)}, u32[]{:S(2)}, u32[]{:S(2)}) async-start(bf16[32,2,56,128]{3,2,1,0:T(8,128)(2,1)} %pack.1), calls=%async_computation.1 | async-start | bytes 1835008 | tf_op jit(solution)/shard_map/all_to_all | solution.py:219
  39.0 36.2 %all-to-all-start = ((bf16[32,56,128]{2,1,0:T(8,128)(2,1)}), bf16[32,56,128]{2,1,0:T(8,128)(2,1)S(1)}, u32[]{:S(2)}, u32[]{:S(2)}) async-start(bf16[32,56,128]{2,1,0:T(8,128)(2,1)} %bitcast_bitcast_fusion), calls=%async_computation | async-start | bytes 917504 | tf_op jit(solution)/shard_map/all_to_all | solution.py:219
  45.0 30.2 %copy-start.3 = (s32[16]{0:T(128)S(1)}, s32[16]{0:T(128)}, u32[]{:S(2)}) copy-start(s32[16]{0:T(128)} %noise.3) | copy-start | bytes 196
  45.1 11.2 %collective-permute-start.4 = (bf16[16,112,128]{2,1,0:T(8,128)(2,1)S(1)}, bf16[16,112,128]{2,1,0:T(8,128)(2,1)S(1)}, u32[]{:S(2)}, u32[]{:S(2)}) collective-permute-start(bf16[16,112,128]{2,1,0:T(8,128)(2,1)S(1)} %bitcast.30), channel_id=1, source_target_pairs={{0,2},{2,4},{4,6},{6,0},{1,3},{3,5},{5,7},{7,1},{8,10},{10,12},{12... | collective-permute-start | bytes 1376264 | tf_op jit(solution)/shard_map/ppermute | solution.py:215
  46.4 22.9 %collective-permute-start.8 = (bf16[16,112,128]{2,1,0:T(8,128)(2,1)S(1)}, bf16[16,112,128]{2,1,0:T(8,128)(2,1)}, u32[]{:S(2)}, u32[]{:S(2)}) collective-permute-start(bf16[16,112,128]{2,1,0:T(8,128)(2,1)S(1)} %bitcast.31), channel_id=1, source_target_pairs={{0,1},{1,0},{2,3},{3,2},{4,5},{5,4},{6,7},{7,6},{8,9},{9,8},{10,11... | collective-permute-start | bytes 1376264 | tf_op jit(solution)/shard_map/ppermute | solution.py:210
  48.8 17.4 %collective-permute-start.7 = (bf16[16,112,128]{2,1,0:T(8,128)(2,1)S(1)}, bf16[16,112,128]{2,1,0:T(8,128)(2,1)}, u32[]{:S(2)}, u32[]{:S(2)}) collective-permute-start(bf16[16,112,128]{2,1,0:T(8,128)(2,1)S(1)} %bitcast.26), channel_id=1, source_target_pairs={{0,2},{2,4},{4,6},{6,0},{1,3},{3,5},{5,7},{7,1},{8,10},{10,12},{12... | collective-permute-start | bytes 1376264 | tf_op jit(solution)/shard_map/ppermute | solution.py:215
  50.9 18.8 %collective-permute-start.9 = (bf16[16,112,128]{2,1,0:T(8,128)(2,1)S(1)}, bf16[16,112,128]{2,1,0:T(8,128)(2,1)}, u32[]{:S(2)}, u32[]{:S(2)}) collective-permute-start(bf16[16,112,128]{2,1,0:T(8,128)(2,1)S(1)} %bitcast.27), channel_id=1, source_target_pairs={{0,1},{1,0},{2,3},{3,2},{4,5},{5,4},{6,7},{7,6},{8,9},{9,8},{10,11... | collective-permute-start | bytes 1376264 | tf_op jit(solution)/shard_map/ppermute | solution.py:210
  51.3 18.5 %collective-permute-start.1 = (bf16[16,112,128]{2,1,0:T(8,128)(2,1)S(1)}, bf16[16,112,128]{2,1,0:T(8,128)(2,1)S(1)}, u32[]{:S(2)}, u32[]{:S(2)}) collective-permute-start(bf16[16,112,128]{2,1,0:T(8,128)(2,1)S(1)} %bitcast.28), channel_id=1, source_target_pairs={{0,6},{2,0},{4,2},{6,4},{1,7},{3,1},{5,3},{7,5},{8,14},{10,8},{12,... | collective-permute-start | bytes 1376264 | tf_op jit(solution)/shard_map/ppermute | solution.py:215
  56.2 16.2 %collective-permute-start = (bf16[16,112,128]{2,1,0:T(8,128)(2,1)S(1)}, bf16[16,112,128]{2,1,0:T(8,128)(2,1)S(1)}, u32[]{:S(2)}, u32[]{:S(2)}) collective-permute-start(bf16[16,112,128]{2,1,0:T(8,128)(2,1)S(1)} %bitcast.32), channel_id=1, source_target_pairs={{0,6},{2,0},{4,2},{6,4},{1,7},{3,1},{5,3},{7,5},{8,14},{10,8},{12,... | collective-permute-start | bytes 1376264 | tf_op jit(solution)/shard_map/ppermute | solution.py:215
  66.2 8.9 %collective-permute-start.10 = (bf16[16,112,128]{2,1,0:T(8,128)(2,1)S(1)}, bf16[16,112,128]{2,1,0:T(8,128)(2,1)}, u32[]{:S(2)}, u32[]{:S(2)}) collective-permute-start(bf16[16,112,128]{2,1,0:T(8,128)(2,1)S(1)} %collective-permute-done.4.refs_2_), channel_id=1, source_target_pairs={{0,1},{1,0},{2,3},{3,2},{4,5},{5,4},{6,7},{7,6},{8,9},{9,8},{10,11... | collective-permute-start | bytes 1376264 | tf_op jit(solution)/shard_map/ppermute | solution.py:210
  69.2 5.9 %collective-permute-start.11 = (bf16[16,112,128]{2,1,0:T(8,128)(2,1)}, bf16[16,112,128]{2,1,0:T(8,128)(2,1)}, u32[]{:S(2)}, u32[]{:S(2)}) collective-permute-start(bf16[16,112,128]{2,1,0:T(8,128)(2,1)} %collective-permute-done.7.refs_3_), channel_id=1, source_target_pairs={{0,1},{1,0},{2,3},{3,2},{4,5},{5,4},{6,7},{7,6},{8,9},{9,8},{10,11... | collective-permute-start | bytes 1376264 | tf_op jit(solution)/shard_map/ppermute | solution.py:210
  69.7 18.6 %collective-permute-start.5 = (bf16[16,112,128]{2,1,0:T(8,128)(2,1)S(1)}, bf16[16,112,128]{2,1,0:T(8,128)(2,1)}, u32[]{:S(2)}, u32[]{:S(2)}) collective-permute-start(bf16[16,112,128]{2,1,0:T(8,128)(2,1)S(1)} %collective-permute-done.4.refs_2_), channel_id=1, source_target_pairs={{0,2},{2,4},{4,6},{6,0},{1,3},{3,5},{5,7},{7,1},{8,10},{10,12},{12... | collective-permute-start | bytes 1376264 | tf_op jit(solution)/shard_map/ppermute | solution.py:215
  69.8 18.5 %collective-permute-start.6 = (bf16[16,112,128]{2,1,0:T(8,128)(2,1)S(1)}, bf16[16,112,128]{2,1,0:T(8,128)(2,1)}, u32[]{:S(2)}, u32[]{:S(2)}) collective-permute-start(bf16[16,112,128]{2,1,0:T(8,128)(2,1)S(1)} %collective-permute-done.1.refs_1_), channel_id=1, source_target_pairs={{0,6},{2,0},{4,2},{6,4},{1,7},{3,1},{5,3},{7,5},{8,14},{10,8},{12,... | collective-permute-start | bytes 1376264 | tf_op jit(solution)/shard_map/ppermute | solution.py:215
  72.4 17.1 %collective-permute-start.3 = (bf16[16,112,128]{2,1,0:T(8,128)(2,1)S(1)}, bf16[16,112,128]{2,1,0:T(8,128)(2,1)}, u32[]{:S(2)}, u32[]{:S(2)}) collective-permute-start(bf16[16,112,128]{2,1,0:T(8,128)(2,1)S(1)} %collective-permute-done.1.refs_1_), channel_id=1, source_target_pairs={{0,1},{1,0},{2,3},{3,2},{4,5},{5,4},{6,7},{7,6},{8,9},{9,8},{10,11... | collective-permute-start | bytes 1376264 | tf_op jit(solution)/shard_map/ppermute | solution.py:210
  75.1 14.4 %collective-permute-start.2 = (bf16[16,112,128]{2,1,0:T(8,128)(2,1)S(1)}, bf16[16,112,128]{2,1,0:T(8,128)(2,1)}, u32[]{:S(2)}, u32[]{:S(2)}) collective-permute-start(bf16[16,112,128]{2,1,0:T(8,128)(2,1)S(1)} %collective-permute-done.refs_0_), channel_id=1, source_target_pairs={{0,1},{1,0},{2,3},{3,2},{4,5},{5,4},{6,7},{7,6},{8,9},{9,8},{10,11... | collective-permute-start | bytes 1376264 | tf_op jit(solution)/shard_map/ppermute | solution.py:210
  87.2 1.0 copy-start.4
  88.2 2.1 %collective-permute-start.12 = (bf16[16,112,128]{2,1,0:T(8,128)(2,1)}, bf16[16,112,128]{2,1,0:T(8,128)(2,1)S(1)}, u32[]{:S(2)}, u32[]{:S(2)}) collective-permute-start(bf16[16,112,128]{2,1,0:T(8,128)(2,1)} %collective-permute-done.5.refs_4_), channel_id=1, source_target_pairs={{0,1},{1,0},{2,3},{3,2},{4,5},{5,4},{6,7},{7,6},{8,9},{9,8},{10,11... | collective-permute-start | bytes 1376264 | tf_op jit(solution)/shard_map/ppermute | solution.py:210
  88.7 2.3 %collective-permute-start.13 = (bf16[16,112,128]{2,1,0:T(8,128)(2,1)}, bf16[16,112,128]{2,1,0:T(8,128)(2,1)S(1)}, u32[]{:S(2)}, u32[]{:S(2)}) collective-permute-start(bf16[16,112,128]{2,1,0:T(8,128)(2,1)} %collective-permute-done.6.refs_5_), channel_id=1, source_target_pairs={{0,1},{1,0},{2,3},{3,2},{4,5},{5,4},{6,7},{7,6},{8,9},{9,8},{10,11... | collective-permute-start | bytes 1376264 | tf_op jit(solution)/shard_map/ppermute | solution.py:210
  91.0 1.2 copy-start.5
where the time goes:
time: 131 us
  waiting for transfers between devices  35.6 us (27%)
  starting transfers between devices  35.3 us (27%)
  Pallas kernels  25.6 us (20%)
  blocking collectives  25 us (19%)
  local copies, waits for them, and re-layouts  6.78 us (5%)
  other arithmetic  1.37 us (1%)
    all_to_all x1, blocking collectives, attention(): back = lax.all_to_all(back, HEAD_AXES, 0, 0, tiled=True)  25 us
    pallas_call x2, Pallas kernels, attend_call(): pl.pallas_call(functools.partial(attend, sources, first, last, groups), o...  24.5 us
    all_to_all x2, waiting for transfers between devices, exchanged(): return lax.all_to_all(blocks, HEAD_AXES, 0, 0, tiled=True)  21.9 us
    all_to_all x2, starting transfers between devices, exchanged(): return lax.all_to_all(blocks, HEAD_AXES, 0, 0, tiled=True)  18.1 us
    ppermute x6, waiting for transfers between devices, shifted(): lax.ppermute(value, 'x', [(i, (i + shift) % size) for i in range(size)])  12.2 us
    ppermute x8, starting transfers between devices, swapped(): return lax.ppermute(value, 'core', [(0, 1), (1, 0)])  9.16 us
    ppermute x6, starting transfers between devices, shifted(): lax.ppermute(value, 'x', [(i, (i + shift) % size) for i in range(size)])  7.97 us
    unnamed x14, local copies, waits for them, and re-layouts  4.34 us
  transfers between devices with their start and end apart: 16, of which 5 were waited for; matrix products, arithmetic and copies ran while one was open for 2% of the time, Pallas kernels for 9%

commit v1 on v0

--- a/solution.py
+++ b/solution.py
@@ -43,7 +43,7 @@
     else:
         m_ref[...] = old_m[...]
         l_ref[...] = old_l[...]
-        fetch = pltpu.make_async_copy(old_acc, acc_ref, done)
+        fetch = pltpu.make_async_copy(old_acc.at[: groups + 1], acc_ref, done)
         fetch.start()
 
     pad = HEAD_DIM - q_ref.shape[1]
@@ -103,7 +103,7 @@
     lax.fori_loop(0, lists[5, 0], step, 0)
 
     if not last:
-        store = pltpu.make_async_copy(acc_ref, acc_out, done)
+        store = pltpu.make_async_copy(acc_ref, acc_out.at[: groups + 1], done)
         store.start()
         store.wait()
 
@@ -134,7 +134,8 @@
         scratch = [pltpu.VMEM(shape, jnp.float32) for shape in state] + work
         out_specs = vmem
     else:
-        out_shape = [jax.ShapeDtypeStruct(shape, jnp.float32) for shape in state]
+        roomy = (8 * (groups + 1), *state[2][1:])
+        out_shape = [jax.ShapeDtypeStruct(shape, jnp.float32) for shape in (*state[:2], roomy)]
         scratch = [pltpu.VMEM(state[2], jnp.float32)] + work
         out_specs = [vmem, vmem, pl.BlockSpec(memory_space=pltpu.HBM)]
     in_specs = [smem, smem] + [vmem] * (1 + len(operands))
@@ -186,22 +187,26 @@
     return value.reshape(value.shape[0], -1, HEAD_DIM).transpose(1, 0, 2)
 
 
-def pack(k_ref, v_ref, o_ref):
-    for h in range(o_ref.shape[0]):
-        lanes = slice(h * HEAD_DIM, (h + 1) * HEAD_DIM)
-        o_ref[h, 0] = k_ref[:, lanes]
-        o_ref[h, 1] = v_ref[:, lanes]
+def pack(k_hbm, v_hbm, o_ref, k_ref, v_ref, done):
+    fetches = [pltpu.make_async_copy(k_hbm, k_ref, done.at[0]), pltpu.make_async_copy(v_hbm, v_ref, done.at[1])]
+    for fetch in fetches:
+        fetch.start()
+    for i, ref in enumerate((k_ref, v_ref)):
+        fetches[i].wait()
+        for h in range(o_ref.shape[0]):
+            o_ref[h, i] = ref[:, h * HEAD_DIM : (h + 1) * HEAD_DIM]
 
 
 def packed(keys, values):
     tokens, width = keys.shape
-    vmem = pl.BlockSpec(memory_space=pltpu.VMEM)
+    hbm = pl.BlockSpec(memory_space=pltpu.HBM)
     return pl.pallas_call(
         pack,
         out_shape=jax.ShapeDtypeStruct((width // HEAD_DIM, 2, tokens, HEAD_DIM), keys.dtype),
-        in_specs=[vmem, vmem],
-        out_specs=vmem,
-        compiler_params=pltpu.CompilerParams(vmem_limit_bytes=8 * 1024 * 1024),
+        in_specs=[hbm, hbm],
+        out_specs=pl.BlockSpec(memory_space=pltpu.VMEM),
+        scratch_shapes=[pltpu.VMEM(keys.shape, keys.dtype)] * 2 + [pltpu.SemaphoreType.DMA((2,))],
+        compiler_params=pltpu.CompilerParams(vmem_limit_bytes=60 * 1024 * 1024),
         name="pack",
     )(keys, values)
 
@@ -231,13 +236,15 @@
     lists = live_pairs(visible)
     head = lax.axis_index(HEAD_AXES)
     gates = lax.dynamic_slice_in_dim(level_gates, head * HEAD_DIM, HEAD_DIM, axis=1)
+    lists, gates = lax.optimization_barrier((lists, gates))
     early = [key, value, key_up, value_up]
-    early = early + [swapped(piece) for piece in early]
+    early += [swapped(piece) for piece in early]
     late = [key_down, value_down]
-    late = late + [swapped(piece) for piece in late]
+    late += [swapped(piece) for piece in late]
     state = attend_call(["two"] * 4, True, False, lists, noise_levels, query, early)
     key_far, value_far, top = lax.optimization_barrier((key_far, value_far, state[0]))
-    late = late + [key_far, value_far, swapped(key_far), swapped(value_far), top, *state[1:], gates]
+    late += [key_far, value_far, swapped(key_far), swapped(value_far)]
+    late += [top, *state[1:], gates]
     out = attend_call(["two"] * 4, False, True, lists, noise_levels, query, late)
     back = out.reshape(lax.axis_size(HEAD_AXES), -1, HEAD_DIM)
     back = lax.all_to_all(back, HEAD_AXES, 0, 0, tiled=True)

time: 131 us -> 128 us (0.977)
  local copies, waits for them, and re-layouts: 6.78 us -> 4.92 us
  starting transfers between devices: 35.3 us -> 33.6 us
    unnamed x14 -> x8, local copies, waits for them, and re-layouts: 4.34 us -> 2.46 us
    ppermute x8, starting transfers between devices: 9.16 us -> 7.64 us  [swapped(): return lax.ppermute(value, 'core', [(0, 1), (1, 0)])]
    all_to_all x2, waiting for transfers between devices: 21.9 us -> 20.6 us  [exchanged(): return lax.all_to_all(blocks, HEAD_AXES, 0, 0, tiled=True)]
  transfers between devices with their start and end apart: 16 -> 16, of which waited for: 5 -> 5; matrix products, arithmetic and copies ran while one was open for 2% -> 3% of each run, Pallas kernels for 9% -> 9%
where the time goes in v1:
time: 128 us
  waiting for transfers between devices  35.5 us (28%)
  starting transfers between devices  33.6 us (26%)
  Pallas kernels  26.6 us (21%)
  blocking collectives  24.5 us (19%)
  local copies, waits for them, and re-layouts  4.92 us (4%)
  other arithmetic  2 us (2%)
    all_to_all x1, blocking collectives, attention(): back = lax.all_to_all(back, HEAD_AXES, 0, 0, tiled=True)  24.5 us
    pallas_call x2, Pallas kernels, attend_call(): pl.pallas_call(functools.partial(attend, sources, first, last, groups), o...  24.3 us
    all_to_all x2, waiting for transfers between devices, exchanged(): return lax.all_to_all(blocks, HEAD_AXES, 0, 0, tiled=True)  20.6 us
    all_to_all x2, starting transfers between devices, exchanged(): return lax.all_to_all(blocks, HEAD_AXES, 0, 0, tiled=True)  18 us
    ppermute x6, waiting for transfers between devices, shifted(): lax.ppermute(value, 'x', [(i, (i + shift) % size) for i in range(size)])  12.7 us
    ppermute x6, starting transfers between devices, shifted(): lax.ppermute(value, 'x', [(i, (i + shift) % size) for i in range(size)])  7.91 us
    ppermute x8, starting transfers between devices, swapped(): return lax.ppermute(value, 'core', [(0, 1), (1, 0)])  7.64 us
  transfers between devices with their start and end apart: 16, of which 5 were waited for; matrix products, arithmetic and copies ran while one was open for 3% of the time, Pallas kernels for 9%

profile of v1, /device:TPU:1, one launch (start us, length us, event | category | flops | bytes accessed | tf_op | source)
XLA Modules:
  0.0 127.9 jit_solution(12390471497158078428)
XLA Ops:
  0.0 2.2 %pack.1 = bf16[32,2,56,128]{3,2,1,0:T(8,128)(2,1)} custom-call(bf16[56,4096]{1,0:T(8,128)(2,1)} %k_hbm.1, bf16[56,4096]{1,0:T(8,128)(2,1)} %v_hbm.1), custom_call_target="tpu_custom_call" | custom-call | tf_op jit(solution)/shard_map/pack/pallas_call | solution.py:203
  2.2 12.0 %all-to-all-start.1 = ((bf16[32,2,56,128]{3,2,1,0:T(8,128)(2,1)}), bf16[32,2,56,128]{3,2,1,0:T(8,128)(2,1)S(1)}, u32[]{:S(2)}, u32[]{:S(2)}) async-start(bf16[32,2,56,128]{3,2,1,0:T(8,128)(2,1)} %pack.1), calls=%async_computation.1 | async-start | bytes 1835008 | tf_op jit(solution)/shard_map/all_to_all | solution.py:224
  14.3 0.7 convert_reduce_fusion.1
  16.5 0.8 bitcast_bitcast_fusion
  17.3 20.6 %all-to-all-done.1 = bf16[32,2,56,128]{3,2,1,0:T(8,128)(2,1)S(1)} async-done(((bf16[32,2,56,128]{3,2,1,0:T(8,128)(2,1)}), bf16[32,2,56,128]{3,2,1,0:T(8,128)(2,1)S(1)}, u32[]{:S(2)}, u32[]{:S(2)}) %all-to-all-start.1) | async-done | bytes 917536 | tf_op jit(solution)/shard_map/all_to_all | solution.py:224
  37.9 6.0 %all-to-all-start = ((bf16[32,56,128]{2,1,0:T(8,128)(2,1)}), bf16[32,56,128]{2,1,0:T(8,128)(2,1)S(1)}, u32[]{:S(2)}, u32[]{:S(2)}) async-start(bf16[32,56,128]{2,1,0:T(8,128)(2,1)} %bitcast_bitcast_fusion), calls=%async_computation | async-start | bytes 917504 | tf_op jit(solution)/shard_map/all_to_all | solution.py:224
  44.0 1.3 %collective-permute-start.4 = (bf16[16,112,128]{2,1,0:T(8,128)(2,1)S(1)}, bf16[16,112,128]{2,1,0:T(8,128)(2,1)S(1)}, u32[]{:S(2)}, u32[]{:S(2)}) collective-permute-start(bf16[16,112,128]{2,1,0:T(8,128)(2,1)S(1)} %bitcast.30), channel_id=1, source_target_pairs={{0,2},{2,4},{4,6},{6,0},{1,3},{3,5},{5,7},{7,1},{8,10},{10,12},{12... | collective-permute-start | bytes 1376264 | tf_op jit(solution)/shard_map/ppermute | solution.py:220
  45.3 2.5 %collective-permute-start.8 = (bf16[16,112,128]{2,1,0:T(8,128)(2,1)S(1)}, bf16[16,112,128]{2,1,0:T(8,128)(2,1)S(1)}, u32[]{:S(2)}, u32[]{:S(2)}) collective-permute-start(bf16[16,112,128]{2,1,0:T(8,128)(2,1)S(1)} %bitcast.31), channel_id=1, source_target_pairs={{0,1},{1,0},{2,3},{3,2},{4,5},{5,4},{6,7},{7,6},{8,9},{9,8},{10,11... | collective-permute-start | bytes 1376264 | tf_op jit(solution)/shard_map/ppermute | solution.py:215
  47.7 1.2 collective-permute-start.7
  49.6 1.5 %collective-permute-start.1 = (bf16[16,112,128]{2,1,0:T(8,128)(2,1)S(1)}, bf16[16,112,128]{2,1,0:T(8,128)(2,1)S(1)}, u32[]{:S(2)}, u32[]{:S(2)}) collective-permute-start(bf16[16,112,128]{2,1,0:T(8,128)(2,1)S(1)} %bitcast.28), channel_id=1, source_target_pairs={{0,6},{2,0},{4,2},{6,4},{1,7},{3,1},{5,3},{7,5},{8,14},{10,8},{12,... | collective-permute-start | bytes 1376264 | tf_op jit(solution)/shard_map/ppermute | solution.py:220
  51.1 4.1 %collective-permute-done.4.refs_2_ = bf16[16,112,128]{2,1,0:T(8,128)(2,1)S(1)} collective-permute-done((bf16[16,112,128]{2,1,0:T(8,128)(2,1)S(1)}, bf16[16,112,128]{2,1,0:T(8,128)(2,1)S(1)}, u32[]{:S(2)}, u32[]{:S(2)}) %collective-permute-start.4) | collective-permute-done | bytes 458784 | tf_op jit(solution)/shard_map/ppermute | solution.py:220
  55.2 1.3 collective-permute-start
  56.4 8.7 %collective-permute-done.7.refs_3_ = bf16[16,112,128]{2,1,0:T(8,128)(2,1)} collective-permute-done((bf16[16,112,128]{2,1,0:T(8,128)(2,1)S(1)}, bf16[16,112,128]{2,1,0:T(8,128)(2,1)}, u32[]{:S(2)}, u32[]{:S(2)}) %collective-permute-start.7) | collective-permute-done | bytes 458784 | tf_op jit(solution)/shard_map/ppermute | solution.py:220
  65.1 3.0 %collective-permute-start.10 = (bf16[16,112,128]{2,1,0:T(8,128)(2,1)S(1)}, bf16[16,112,128]{2,1,0:T(8,128)(2,1)}, u32[]{:S(2)}, u32[]{:S(2)}) collective-permute-start(bf16[16,112,128]{2,1,0:T(8,128)(2,1)S(1)} %collective-permute-done.4.refs_2_), channel_id=1, source_target_pairs={{0,1},{1,0},{2,3},{3,2},{4,5},{5,4},{6,7},{7,6},{8,9},{9,8},{10,11... | collective-permute-start | bytes 1376264 | tf_op jit(solution)/shard_map/ppermute | solution.py:215
  68.1 0.8 copy-done.1
  69.2 0.7 constant_dynamic-slice_fusion.refs_11_
  69.9 2.7 %collective-permute-start.6 = (bf16[16,112,128]{2,1,0:T(8,128)(2,1)S(1)}, bf16[16,112,128]{2,1,0:T(8,128)(2,1)}, u32[]{:S(2)}, u32[]{:S(2)}) collective-permute-start(bf16[16,112,128]{2,1,0:T(8,128)(2,1)S(1)} %collective-permute-done.1.refs_1_), channel_id=1, source_target_pairs={{0,6},{2,0},{4,2},{6,4},{1,7},{3,1},{5,3},{7,5},{8,14},{10,8},{12,... | collective-permute-start | bytes 1376264 | tf_op jit(solution)/shard_map/ppermute | solution.py:220
  72.6 1.1 collective-permute-start.3
  73.7 1.0 copy-done.2
  75.4 11.9 %attend_first.1 = (f32[17,1,128]{2,1,0:T(1,128)S(1)}, f32[17,1,128]{2,1,0:T(1,128)S(1)}, f32[136,128,128]{2,1,0:T(8,128)S(1)}) custom-call(s32[6,79]{1,0:T(8,128)S(1)} %stack.17.lists, s32[16]{0:T(128)S(1)} %copy-done.3, bf16[16,112,128]{2,1,0:T(8,128)(2,1)S(1)} %bitcast.34, bf16[16,112,128]{2,1,0:T(8,128)(2,1)S(1)} %bitcast.33, ...), custom_call_target="tpu_custom_call" | custom-call | flops 10481565696 | bytes 3670016 | tf_op jit(solution)/shard_map/attend_first/pallas_call | solution.py:144
  88.0 1.5 %collective-permute-done.12.refs_6_ = bf16[16,112,128]{2,1,0:T(8,128)(2,1)S(1)} collective-permute-done((bf16[16,112,128]{2,1,0:T(8,128)(2,1)}, bf16[16,112,128]{2,1,0:T(8,128)(2,1)S(1)}, u32[]{:S(2)}, u32[]{:S(2)}) %collective-permute-start.12) | collective-permute-done | bytes 458784 | tf_op jit(solution)/shard_map/ppermute | solution.py:215
  90.2 12.4 %attend_last.1 = bf16[16,112,128]{2,1,0:T(8,128)(2,1)S(1)} custom-call(s32[6,79]{1,0:T(8,128)S(1)} %stack.17.lists, s32[16]{0:T(128)S(1)} %copy-done.3, bf16[16,112,128]{2,1,0:T(8,128)(2,1)S(1)} %bitcast.35, bf16[16,112,128]{2,1,0:T(8,128)(2,1)S(1)} %collective-permute-done.refs_0_, bf16[16,112,128]{2,1,0:T(8,128)(2,1)S(1)} %collective-permute-done.1.refs_1_, ...), custom_call_target="tpu_custom_call" | custom-call | flops 10481565696 | bytes 3670016 | tf_op jit(solution)/shard_map/attend_last/pallas_call | solution.py:144
  102.6 24.5 %all_to_all.15 = bf16[32,56,128]{2,1,0:T(8,128)(2,1)S(1)} all-to-all(bf16[32,56,128]{2,1,0:T(8,128)(2,1)S(1)} %bitcast.36), channel_id=1, replica_groups=mesh['z'=8,'yh'=2,'yl'=2,'x'=4,'core'=2] {'z','yh','yl'}, dimensions={0} | all-to-all | bytes 917504 | tf_op jit(solution)/shard_map/all_to_all | solution.py:250
  127.1 0.8 copy_bitcast_fusion
  (36 shorter events, 3.8 us)
Async XLA Ops:
  0.0 16.5 %copy-start = (bf16[56,4096]{1,0:T(8,128)(2,1)S(1)}, bf16[56,4096]{1,0:T(8,128)(2,1)}, u32[]{:S(2)}) copy-start(bf16[56,4096]{1,0:T(8,128)(2,1)} %param.6) | copy-start | bytes 1376260
  2.2 35.7 %all-to-all-start.1 = ((bf16[32,2,56,128]{3,2,1,0:T(8,128)(2,1)}), bf16[32,2,56,128]{3,2,1,0:T(8,128)(2,1)S(1)}, u32[]{:S(2)}, u32[]{:S(2)}) async-start(bf16[32,2,56,128]{3,2,1,0:T(8,128)(2,1)} %pack.1), calls=%async_computation.1 | async-start | bytes 1835008 | tf_op jit(solution)/shard_map/all_to_all | solution.py:224
  37.9 35.8 %all-to-all-start = ((bf16[32,56,128]{2,1,0:T(8,128)(2,1)}), bf16[32,56,128]{2,1,0:T(8,128)(2,1)S(1)}, u32[]{:S(2)}, u32[]{:S(2)}) async-start(bf16[32,56,128]{2,1,0:T(8,128)(2,1)} %bitcast_bitcast_fusion), calls=%async_computation | async-start | bytes 917504 | tf_op jit(solution)/shard_map/all_to_all | solution.py:224
  44.0 11.2 %collective-permute-start.4 = (bf16[16,112,128]{2,1,0:T(8,128)(2,1)S(1)}, bf16[16,112,128]{2,1,0:T(8,128)(2,1)S(1)}, u32[]{:S(2)}, u32[]{:S(2)}) collective-permute-start(bf16[16,112,128]{2,1,0:T(8,128)(2,1)S(1)} %bitcast.30), channel_id=1, source_target_pairs={{0,2},{2,4},{4,6},{6,0},{1,3},{3,5},{5,7},{7,1},{8,10},{10,12},{12... | collective-permute-start | bytes 1376264 | tf_op jit(solution)/shard_map/ppermute | solution.py:220
  45.3 22.9 %collective-permute-start.8 = (bf16[16,112,128]{2,1,0:T(8,128)(2,1)S(1)}, bf16[16,112,128]{2,1,0:T(8,128)(2,1)S(1)}, u32[]{:S(2)}, u32[]{:S(2)}) collective-permute-start(bf16[16,112,128]{2,1,0:T(8,128)(2,1)S(1)} %bitcast.31), channel_id=1, source_target_pairs={{0,1},{1,0},{2,3},{3,2},{4,5},{5,4},{6,7},{7,6},{8,9},{9,8},{10,11... | collective-permute-start | bytes 1376264 | tf_op jit(solution)/shard_map/ppermute | solution.py:215
  47.7 17.4 %collective-permute-start.7 = (bf16[16,112,128]{2,1,0:T(8,128)(2,1)S(1)}, bf16[16,112,128]{2,1,0:T(8,128)(2,1)}, u32[]{:S(2)}, u32[]{:S(2)}) collective-permute-start(bf16[16,112,128]{2,1,0:T(8,128)(2,1)S(1)} %bitcast.26), channel_id=1, source_target_pairs={{0,2},{2,4},{4,6},{6,0},{1,3},{3,5},{5,7},{7,1},{8,10},{10,12},{12... | collective-permute-start | bytes 1376264 | tf_op jit(solution)/shard_map/ppermute | solution.py:220
  49.3 20.6 %collective-permute-start.9 = (bf16[16,112,128]{2,1,0:T(8,128)(2,1)S(1)}, bf16[16,112,128]{2,1,0:T(8,128)(2,1)}, u32[]{:S(2)}, u32[]{:S(2)}) collective-permute-start(bf16[16,112,128]{2,1,0:T(8,128)(2,1)S(1)} %bitcast.27), channel_id=1, source_target_pairs={{0,1},{1,0},{2,3},{3,2},{4,5},{5,4},{6,7},{7,6},{8,9},{9,8},{10,11... | collective-permute-start | bytes 1376264 | tf_op jit(solution)/shard_map/ppermute | solution.py:215
  49.6 20.3 %collective-permute-start.1 = (bf16[16,112,128]{2,1,0:T(8,128)(2,1)S(1)}, bf16[16,112,128]{2,1,0:T(8,128)(2,1)S(1)}, u32[]{:S(2)}, u32[]{:S(2)}) collective-permute-start(bf16[16,112,128]{2,1,0:T(8,128)(2,1)S(1)} %bitcast.28), channel_id=1, source_target_pairs={{0,6},{2,0},{4,2},{6,4},{1,7},{3,1},{5,3},{7,5},{8,14},{10,8},{12,... | collective-permute-start | bytes 1376264 | tf_op jit(solution)/shard_map/ppermute | solution.py:220
  55.2 17.4 %collective-permute-start = (bf16[16,112,128]{2,1,0:T(8,128)(2,1)S(1)}, bf16[16,112,128]{2,1,0:T(8,128)(2,1)S(1)}, u32[]{:S(2)}, u32[]{:S(2)}) collective-permute-start(bf16[16,112,128]{2,1,0:T(8,128)(2,1)S(1)} %bitcast.32), channel_id=1, source_target_pairs={{0,6},{2,0},{4,2},{6,4},{1,7},{3,1},{5,3},{7,5},{8,14},{10,8},{12,... | collective-permute-start | bytes 1376264 | tf_op jit(solution)/shard_map/ppermute | solution.py:220
  65.1 8.5 %collective-permute-start.10 = (bf16[16,112,128]{2,1,0:T(8,128)(2,1)S(1)}, bf16[16,112,128]{2,1,0:T(8,128)(2,1)}, u32[]{:S(2)}, u32[]{:S(2)}) collective-permute-start(bf16[16,112,128]{2,1,0:T(8,128)(2,1)S(1)} %collective-permute-done.4.refs_2_), channel_id=1, source_target_pairs={{0,1},{1,0},{2,3},{3,2},{4,5},{5,4},{6,7},{7,6},{8,9},{9,8},{10,11... | collective-permute-start | bytes 1376264 | tf_op jit(solution)/shard_map/ppermute | solution.py:215
  68.1 0.8 copy-start.1
  68.9 4.8 %collective-permute-start.11 = (bf16[16,112,128]{2,1,0:T(8,128)(2,1)}, bf16[16,112,128]{2,1,0:T(8,128)(2,1)}, u32[]{:S(2)}, u32[]{:S(2)}) collective-permute-start(bf16[16,112,128]{2,1,0:T(8,128)(2,1)} %collective-permute-done.7.refs_3_), channel_id=1, source_target_pairs={{0,1},{1,0},{2,3},{3,2},{4,5},{5,4},{6,7},{7,6},{8,9},{9,8},{10,11... | collective-permute-start | bytes 1376264 | tf_op jit(solution)/shard_map/ppermute | solution.py:215
  69.9 17.5 %collective-permute-start.5 = (bf16[16,112,128]{2,1,0:T(8,128)(2,1)S(1)}, bf16[16,112,128]{2,1,0:T(8,128)(2,1)}, u32[]{:S(2)}, u32[]{:S(2)}) collective-permute-start(bf16[16,112,128]{2,1,0:T(8,128)(2,1)S(1)} %collective-permute-done.4.refs_2_), channel_id=1, source_target_pairs={{0,2},{2,4},{4,6},{6,0},{1,3},{3,5},{5,7},{7,1},{8,10},{10,12},{12... | collective-permute-start | bytes 1376264 | tf_op jit(solution)/shard_map/ppermute | solution.py:220
  69.9 17.5 %collective-permute-start.6 = (bf16[16,112,128]{2,1,0:T(8,128)(2,1)S(1)}, bf16[16,112,128]{2,1,0:T(8,128)(2,1)}, u32[]{:S(2)}, u32[]{:S(2)}) collective-permute-start(bf16[16,112,128]{2,1,0:T(8,128)(2,1)S(1)} %collective-permute-done.1.refs_1_), channel_id=1, source_target_pairs={{0,6},{2,0},{4,2},{6,4},{1,7},{3,1},{5,3},{7,5},{8,14},{10,8},{12,... | collective-permute-start | bytes 1376264 | tf_op jit(solution)/shard_map/ppermute | solution.py:220
  72.6 15.4 %collective-permute-start.3 = (bf16[16,112,128]{2,1,0:T(8,128)(2,1)S(1)}, bf16[16,112,128]{2,1,0:T(8,128)(2,1)}, u32[]{:S(2)}, u32[]{:S(2)}) collective-permute-start(bf16[16,112,128]{2,1,0:T(8,128)(2,1)S(1)} %collective-permute-done.1.refs_1_), channel_id=1, source_target_pairs={{0,1},{1,0},{2,3},{3,2},{4,5},{5,4},{6,7},{7,6},{8,9},{9,8},{10,11... | collective-permute-start | bytes 1376264 | tf_op jit(solution)/shard_map/ppermute | solution.py:215
  73.6 14.3 %collective-permute-start.2 = (bf16[16,112,128]{2,1,0:T(8,128)(2,1)S(1)}, bf16[16,112,128]{2,1,0:T(8,128)(2,1)}, u32[]{:S(2)}, u32[]{:S(2)}) collective-permute-start(bf16[16,112,128]{2,1,0:T(8,128)(2,1)S(1)} %collective-permute-done.refs_0_), channel_id=1, source_target_pairs={{0,1},{1,0},{2,3},{3,2},{4,5},{5,4},{6,7},{7,6},{8,9},{9,8},{10,11... | collective-permute-start | bytes 1376264 | tf_op jit(solution)/shard_map/ppermute | solution.py:215
  73.7 1.0 copy-start.2
  74.8 0.7 copy-start.3
  87.4 2.2 %collective-permute-start.12 = (bf16[16,112,128]{2,1,0:T(8,128)(2,1)}, bf16[16,112,128]{2,1,0:T(8,128)(2,1)S(1)}, u32[]{:S(2)}, u32[]{:S(2)}) collective-permute-start(bf16[16,112,128]{2,1,0:T(8,128)(2,1)} %collective-permute-done.5.refs_4_), channel_id=1, source_target_pairs={{0,1},{1,0},{2,3},{3,2},{4,5},{5,4},{6,7},{7,6},{8,9},{9,8},{10,11... | collective-permute-start | bytes 1376264 | tf_op jit(solution)/shard_map/ppermute | solution.py:215
  87.9 2.3 %collective-permute-start.13 = (bf16[16,112,128]{2,1,0:T(8,128)(2,1)}, bf16[16,112,128]{2,1,0:T(8,128)(2,1)S(1)}, u32[]{:S(2)}, u32[]{:S(2)}) collective-permute-start(bf16[16,112,128]{2,1,0:T(8,128)(2,1)} %collective-permute-done.6.refs_5_), channel_id=1, source_target_pairs={{0,1},{1,0},{2,3},{3,2},{4,5},{5,4},{6,7},{7,6},{8,9},{9,8},{10,11... | collective-permute-start | bytes 1376264 | tf_op jit(solution)/shard_map/ppermute | solution.py:215

commit v2 on v1

--- a/solution.py
+++ b/solution.py
@@ -14,11 +14,11 @@
 AXES = ("z", "yh", "yl", "x", "core")
 HEAD_AXES = ("z", "yh", "yl")
 NEGATIVE = -1e30
-UNROLL = 4
+UNROLL = 9
 TO_EXP2 = math.log2(math.e) / math.sqrt(HEAD_DIM)
 
 
-def attend(sources, first, last, groups, lists, noise, q_ref, *refs):
+def attend(sources, first, last, groups, lists, q_ref, *refs):
     refs = list(refs)
     keys, values = [], []
     for kind in sources:
@@ -110,7 +110,7 @@
     if last:
 
         def finish(c, carry):
-            gate = gate_ref[pl.ds(noise[c], 1), :]
+            gate = gate_ref[pl.ds(lists[6, c], 1), :]
             ratio = (acc_ref[c] / l_ref[c]).T[: q_ref.shape[1]]
             o_ref[c] = (ratio * gate).astype(o_ref.dtype)
             return carry
@@ -118,7 +118,7 @@
         lax.fori_loop(0, groups, finish, 0, unroll=4)
 
 
-def attend_call(sources, first, last, lists, noise, query, operands):
+def attend_call(sources, first, last, lists, query, operands):
     groups, rows, _ = query.shape
     width = len(sources) * rows
     blocks = groups * (groups + 1) // 2
@@ -138,7 +138,7 @@
         out_shape = [jax.ShapeDtypeStruct(shape, jnp.float32) for shape in (*state[:2], roomy)]
         scratch = [pltpu.VMEM(state[2], jnp.float32)] + work
         out_specs = [vmem, vmem, pl.BlockSpec(memory_space=pltpu.HBM)]
-    in_specs = [smem, smem] + [vmem] * (1 + len(operands))
+    in_specs = [smem] + [vmem] * (1 + len(operands))
     if not first:
         in_specs[-2 if last else -1] = pl.BlockSpec(memory_space=pltpu.HBM)
     return pl.pallas_call(
@@ -154,10 +154,10 @@
             transcendentals=blocks * rows * width,
         ),
         name="attend_last" if last else "attend_first",
-    )(lists, noise, query, *operands)
-
-
-def live_pairs(visible):
+    )(lists, query, *operands)
+
+
+def live_pairs(visible, noise_levels):
     groups = visible.shape[0]
     ids = jnp.arange(groups, dtype=jnp.int32)
     c, e = ids[:, None], ids[None, :]
@@ -180,7 +180,8 @@
         rows.append((query, key, jnp.where(found, query, groups)))
     (q0, key, s0), (q1, _, s1) = rows
     steps = jnp.broadcast_to((total + UNROLL - 1) // UNROLL, places.shape)
-    return jnp.stack([q0, q1, key, s0, s1, steps])
+    noise = jnp.pad(noise_levels, (0, length - groups))
+    return jnp.stack([q0, q1, key, s0, s1, steps, noise])
 
 
 def to_heads(value):
@@ -229,23 +230,23 @@
     pair = exchanged(packed(key_vectors, value_vectors))
     key = pair[:, 0].reshape(groups, -1, HEAD_DIM)
     value = pair[:, 1].reshape(groups, -1, HEAD_DIM)
-    query = exchanged(to_heads(queries)).reshape(groups, -1, HEAD_DIM)
+    lists = live_pairs(visible, noise_levels)
+    head = lax.axis_index(HEAD_AXES)
+    gates = lax.dynamic_slice_in_dim(level_gates, head * HEAD_DIM, HEAD_DIM, axis=1)
+    blocks, lists, gates = lax.optimization_barrier((to_heads(queries), lists, gates))
+    query = exchanged(blocks).reshape(groups, -1, HEAD_DIM)
     key_up, key_down = shifted(key, 1), shifted(key, -1)
     value_up, value_down = shifted(value, 1), shifted(value, -1)
     key_far, value_far = shifted(key_up, 1), shifted(value_down, -1)
-    lists = live_pairs(visible)
-    head = lax.axis_index(HEAD_AXES)
-    gates = lax.dynamic_slice_in_dim(level_gates, head * HEAD_DIM, HEAD_DIM, axis=1)
-    lists, gates = lax.optimization_barrier((lists, gates))
     early = [key, value, key_up, value_up]
     early += [swapped(piece) for piece in early]
     late = [key_down, value_down]
     late += [swapped(piece) for piece in late]
-    state = attend_call(["two"] * 4, True, False, lists, noise_levels, query, early)
+    state = attend_call(["two"] * 4, True, False, lists, query, early)
     key_far, value_far, top = lax.optimization_barrier((key_far, value_far, state[0]))
     late += [key_far, value_far, swapped(key_far), swapped(value_far)]
     late += [top, *state[1:], gates]
-    out = attend_call(["two"] * 4, False, True, lists, noise_levels, query, late)
+    out = attend_call(["two"] * 4, False, True, lists, query, late)
     back = out.reshape(lax.axis_size(HEAD_AXES), -1, HEAD_DIM)
     back = lax.all_to_all(back, HEAD_AXES, 0, 0, tiled=True)
     return back.transpose(1, 0, 2).reshape(queries.shape)

time: 128 us -> 130 us (1.016); the launches traced: 128 us -> 128 us
  local copies, waits for them, and re-layouts: 4.92 us -> 6.68 us
  Pallas kernels: 26.6 us -> 24.9 us
    ppermute x8, starting transfers between devices: 7.64 us -> 9.94 us  [swapped(): return lax.ppermute(value, 'core', [(0, 1), (1, 0)])]
    pallas_call x2, Pallas kernels: 24.3 us -> 22.7 us  [attend_call(): pl.pallas_call(functools.partial(attend, sources, first, last, groups), o...]
    unnamed x8 -> x10, local copies, waits for them, and re-layouts: 2.46 us -> 3.57 us
  transfers between devices with their start and end apart: 16 -> 16, of which waited for: 5 -> 5; matrix products, arithmetic and copies ran while one was open for 3% -> 3% of each run, Pallas kernels for 9% -> 8%
where the time goes in v2:
time: 130 us; the launch traced here: 128 us
  waiting for transfers between devices  35.3 us (27%)
  starting transfers between devices  33.9 us (26%)
  Pallas kernels  24.9 us (19%)
  blocking collectives  24.8 us (19%)
  local copies, waits for them, and re-layouts  6.68 us (5%)
  other arithmetic  1.97 us (2%)
    all_to_all x1, blocking collectives, attention(): back = lax.all_to_all(back, HEAD_AXES, 0, 0, tiled=True)  24.8 us
    pallas_call x2, Pallas kernels, attend_call(): pl.pallas_call(functools.partial(attend, sources, first, last, groups), o...  22.7 us
    all_to_all x2, waiting for transfers between devices, exchanged(): return lax.all_to_all(blocks, HEAD_AXES, 0, 0, tiled=True)  20 us
    all_to_all x2, starting transfers between devices, exchanged(): return lax.all_to_all(blocks, HEAD_AXES, 0, 0, tiled=True)  17 us
    ppermute x6, waiting for transfers between devices, shifted(): lax.ppermute(value, 'x', [(i, (i + shift) % size) for i in range(size)])  13 us
    ppermute x8, starting transfers between devices, swapped(): return lax.ppermute(value, 'core', [(0, 1), (1, 0)])  9.94 us
    ppermute x6, starting transfers between devices, shifted(): lax.ppermute(value, 'x', [(i, (i + shift) % size) for i in range(size)])  6.9 us
    unnamed x10, local copies, waits for them, and re-layouts  3.57 us
  transfers between devices with their start and end apart: 16, of which 5 were waited for; matrix products, arithmetic and copies ran while one was open for 3% of the time, Pallas kernels for 8%

profile of v2, /device:TPU:1, one launch (start us, length us, event | category | flops | bytes accessed | tf_op | source)
XLA Modules:
  0.0 128.3 jit_solution(14812032087955574064)
XLA Ops:
  0.0 2.2 %pack.1 = bf16[32,2,56,128]{3,2,1,0:T(8,128)(2,1)} custom-call(bf16[56,4096]{1,0:T(8,128)(2,1)} %k_hbm.1, bf16[56,4096]{1,0:T(8,128)(2,1)} %v_hbm.1), custom_call_target="tpu_custom_call" | custom-call | tf_op jit(solution)/shard_map/pack/pallas_call | solution.py:204
  2.2 12.0 %all-to-all-start.1 = ((bf16[32,2,56,128]{3,2,1,0:T(8,128)(2,1)}), bf16[32,2,56,128]{3,2,1,0:T(8,128)(2,1)S(1)}, u32[]{:S(2)}, u32[]{:S(2)}) async-start(bf16[32,2,56,128]{3,2,1,0:T(8,128)(2,1)} %pack.1), calls=%async_computation.1 | async-start | bytes 1835008 | tf_op jit(solution)/shard_map/all_to_all | solution.py:225
  17.0 0.8 bitcast_bitcast_fusion
  17.9 20.0 %all-to-all-done.1 = bf16[32,2,56,128]{3,2,1,0:T(8,128)(2,1)S(1)} async-done(((bf16[32,2,56,128]{3,2,1,0:T(8,128)(2,1)}), bf16[32,2,56,128]{3,2,1,0:T(8,128)(2,1)S(1)}, u32[]{:S(2)}, u32[]{:S(2)}) %all-to-all-start.1) | async-done | bytes 917536 | tf_op jit(solution)/shard_map/all_to_all | solution.py:225
  38.0 1.3 %collective-permute-start.4 = (bf16[16,112,128]{2,1,0:T(8,128)(2,1)S(1)}, bf16[16,112,128]{2,1,0:T(8,128)(2,1)S(1)}, u32[]{:S(2)}, u32[]{:S(2)}) collective-permute-start(bf16[16,112,128]{2,1,0:T(8,128)(2,1)S(1)} %bitcast.32), channel_id=1, source_target_pairs={{0,2},{2,4},{4,6},{6,0},{1,3},{3,5},{5,7},{7,1},{8,10},{10,12},{12... | collective-permute-start | bytes 1376264 | tf_op jit(solution)/shard_map/ppermute | solution.py:221
  39.3 3.2 %collective-permute-start.8 = (bf16[16,112,128]{2,1,0:T(8,128)(2,1)S(1)}, bf16[16,112,128]{2,1,0:T(8,128)(2,1)S(1)}, u32[]{:S(2)}, u32[]{:S(2)}) collective-permute-start(bf16[16,112,128]{2,1,0:T(8,128)(2,1)S(1)} %bitcast.33), channel_id=1, source_target_pairs={{0,1},{1,0},{2,3},{3,2},{4,5},{5,4},{6,7},{7,6},{8,9},{9,8},{10,11... | collective-permute-start | bytes 1376264 | tf_op jit(solution)/shard_map/ppermute | solution.py:216
  42.4 1.2 collective-permute-start.7
  44.9 5.0 %all-to-all-start = ((bf16[32,56,128]{2,1,0:T(8,128)(2,1)}), bf16[32,56,128]{2,1,0:T(8,128)(2,1)S(1)}, u32[]{:S(2)}, u32[]{:S(2)}) async-start(bf16[32,56,128]{2,1,0:T(8,128)(2,1)} %bitcast_bitcast_fusion), calls=%async_computation | async-start | bytes 917504 | tf_op jit(solution)/shard_map/all_to_all | solution.py:225
  50.6 1.5 %collective-permute-start.1 = (bf16[16,112,128]{2,1,0:T(8,128)(2,1)S(1)}, bf16[16,112,128]{2,1,0:T(8,128)(2,1)}, u32[]{:S(2)}, u32[]{:S(2)}) collective-permute-start(bf16[16,112,128]{2,1,0:T(8,128)(2,1)S(1)} %bitcast.30), channel_id=1, source_target_pairs={{0,6},{2,0},{4,2},{6,4},{1,7},{3,1},{5,3},{7,5},{8,14},{10,8},{12,... | collective-permute-start | bytes 1376264 | tf_op jit(solution)/shard_map/ppermute | solution.py:221
  52.3 6.0 %collective-permute-done.7.refs_3_ = bf16[16,112,128]{2,1,0:T(8,128)(2,1)S(1)} collective-permute-done((bf16[16,112,128]{2,1,0:T(8,128)(2,1)S(1)}, bf16[16,112,128]{2,1,0:T(8,128)(2,1)S(1)}, u32[]{:S(2)}, u32[]{:S(2)}) %collective-permute-start.7) | collective-permute-done | bytes 458784 | tf_op jit(solution)/shard_map/ppermute | solution.py:221
  58.3 3.7 %collective-permute-start.10 = (bf16[16,112,128]{2,1,0:T(8,128)(2,1)S(1)}, bf16[16,112,128]{2,1,0:T(8,128)(2,1)S(1)}, u32[]{:S(2)}, u32[]{:S(2)}) collective-permute-start(bf16[16,112,128]{2,1,0:T(8,128)(2,1)S(1)} %collective-permute-done.4.refs_2_), channel_id=1, source_target_pairs={{0,1},{1,0},{2,3},{3,2},{4,5},{5,4},{6,7},{7,6},{8,9},{9,8},{10,11... | collective-permute-start | bytes 1376264 | tf_op jit(solution)/shard_map/ppermute | solution.py:216
  62.1 0.8 copy-done.1
  62.8 2.7 %collective-permute-start.6 = (bf16[16,112,128]{2,1,0:T(8,128)(2,1)}, bf16[16,112,128]{2,1,0:T(8,128)(2,1)}, u32[]{:S(2)}, u32[]{:S(2)}) collective-permute-start(bf16[16,112,128]{2,1,0:T(8,128)(2,1)} %collective-permute-done.1.refs_1_), channel_id=1, source_target_pairs={{0,6},{2,0},{4,2},{6,4},{1,7},{3,1},{5,3},{7,5},{8,14},{10,8},{12,... | collective-permute-start | bytes 1376264 | tf_op jit(solution)/shard_map/ppermute | solution.py:221
  65.5 7.0 %collective-permute-done.refs_0_ = bf16[16,112,128]{2,1,0:T(8,128)(2,1)} collective-permute-done((bf16[16,112,128]{2,1,0:T(8,128)(2,1)S(1)}, bf16[16,112,128]{2,1,0:T(8,128)(2,1)}, u32[]{:S(2)}, u32[]{:S(2)}) %collective-permute-start) | collective-permute-done | bytes 458784 | tf_op jit(solution)/shard_map/ppermute | solution.py:221
  72.5 1.5 %collective-permute-start.3 = (bf16[16,112,128]{2,1,0:T(8,128)(2,1)}, bf16[16,112,128]{2,1,0:T(8,128)(2,1)}, u32[]{:S(2)}, u32[]{:S(2)}) collective-permute-start(bf16[16,112,128]{2,1,0:T(8,128)(2,1)} %collective-permute-done.1.refs_1_), channel_id=1, source_target_pairs={{0,1},{1,0},{2,3},{3,2},{4,5},{5,4},{6,7},{7,6},{8,9},{9,8},{10,11... | collective-permute-start | bytes 1376264 | tf_op jit(solution)/shard_map/ppermute | solution.py:216
  74.0 0.8 copy-done.3
  74.8 1.0 copy-done.2
  75.8 1.0 copy-done.4
  76.8 10.8 %attend_first.1 = (f32[17,1,128]{2,1,0:T(1,128)S(1)}, f32[17,1,128]{2,1,0:T(1,128)S(1)}, f32[136,128,128]{2,1,0:T(8,128)S(1)}) custom-call(s32[7,89]{1,0:T(8,128)S(1)} %stack.21.lists, bf16[16,112,128]{2,1,0:T(8,128)(2,1)S(1)} %bitcast.36, bf16[16,112,128]{2,1,0:T(8,128)(2,1)S(1)} %bitcast.35, bf16[16,112,128]{2,1,0:T(8,128)(2,1)S(1)} %bitcast.31, ...), custom_call_target="tpu_custom_call" | custom-call | flops 10481565696 | bytes 3670016 | tf_op jit(solution)/shard_map/attend_first/pallas_call | solution.py:144
  87.6 0.8 collective-permute-start.12
  88.5 1.5 %collective-permute-done.12.refs_6_ = bf16[16,112,128]{2,1,0:T(8,128)(2,1)S(1)} collective-permute-done((bf16[16,112,128]{2,1,0:T(8,128)(2,1)}, bf16[16,112,128]{2,1,0:T(8,128)(2,1)S(1)}, u32[]{:S(2)}, u32[]{:S(2)}) %collective-permute-start.12) | collective-permute-done | bytes 458784 | tf_op jit(solution)/shard_map/ppermute | solution.py:216
  90.7 12.0 %attend_last.1 = bf16[16,112,128]{2,1,0:T(8,128)(2,1)S(1)} custom-call(s32[7,89]{1,0:T(8,128)S(1)} %stack.21.lists, bf16[16,112,128]{2,1,0:T(8,128)(2,1)S(1)} %bitcast.37, bf16[16,112,128]{2,1,0:T(8,128)(2,1)} %collective-permute-done.refs_0_, bf16[16,112,128]{2,1,0:T(8,128)(2,1)} %collective-permute-done.1.refs_1_, ...), custom_call_target="tpu_custom_call" | custom-call | flops 10481565696 | bytes 3670016 | tf_op jit(solution)/shard_map/attend_last/pallas_call | solution.py:144
  102.7 24.8 %all_to_all.15 = bf16[32,56,128]{2,1,0:T(8,128)(2,1)S(1)} all-to-all(bf16[32,56,128]{2,1,0:T(8,128)(2,1)S(1)} %bitcast.38), channel_id=1, replica_groups=mesh['z'=8,'yh'=2,'yl'=2,'x'=4,'core'=2] {'z','yh','yl'}, dimensions={0} | all-to-all | bytes 917504 | tf_op jit(solution)/shard_map/all_to_all | solution.py:251
  127.5 0.8 copy_bitcast_fusion
  (39 shorter events, 5.1 us)
Async XLA Ops:
  0.0 17.0 %copy-start = (bf16[56,4096]{1,0:T(8,128)(2,1)S(1)}, bf16[56,4096]{1,0:T(8,128)(2,1)}, u32[]{:S(2)}) copy-start(bf16[56,4096]{1,0:T(8,128)(2,1)} %param.6) | copy-start | bytes 1376260
  2.2 35.7 %all-to-all-start.1 = ((bf16[32,2,56,128]{3,2,1,0:T(8,128)(2,1)}), bf16[32,2,56,128]{3,2,1,0:T(8,128)(2,1)S(1)}, u32[]{:S(2)}, u32[]{:S(2)}) async-start(bf16[32,2,56,128]{3,2,1,0:T(8,128)(2,1)} %pack.1), calls=%async_computation.1 | async-start | bytes 1835008 | tf_op jit(solution)/shard_map/all_to_all | solution.py:225
  38.0 14.1 %collective-permute-start.4 = (bf16[16,112,128]{2,1,0:T(8,128)(2,1)S(1)}, bf16[16,112,128]{2,1,0:T(8,128)(2,1)S(1)}, u32[]{:S(2)}, u32[]{:S(2)}) collective-permute-start(bf16[16,112,128]{2,1,0:T(8,128)(2,1)S(1)} %bitcast.32), channel_id=1, source_target_pairs={{0,2},{2,4},{4,6},{6,0},{1,3},{3,5},{5,7},{7,1},{8,10},{10,12},{12... | collective-permute-start | bytes 1376264 | tf_op jit(solution)/shard_map/ppermute | solution.py:221
  39.3 22.8 %collective-permute-start.8 = (bf16[16,112,128]{2,1,0:T(8,128)(2,1)S(1)}, bf16[16,112,128]{2,1,0:T(8,128)(2,1)S(1)}, u32[]{:S(2)}, u32[]{:S(2)}) collective-permute-start(bf16[16,112,128]{2,1,0:T(8,128)(2,1)S(1)} %bitcast.33), channel_id=1, source_target_pairs={{0,1},{1,0},{2,3},{3,2},{4,5},{5,4},{6,7},{7,6},{8,9},{9,8},{10,11... | collective-permute-start | bytes 1376264 | tf_op jit(solution)/shard_map/ppermute | solution.py:216
  42.4 15.8 %collective-permute-start.7 = (bf16[16,112,128]{2,1,0:T(8,128)(2,1)S(1)}, bf16[16,112,128]{2,1,0:T(8,128)(2,1)S(1)}, u32[]{:S(2)}, u32[]{:S(2)}) collective-permute-start(bf16[16,112,128]{2,1,0:T(8,128)(2,1)S(1)} %bitcast.28), channel_id=1, source_target_pairs={{0,2},{2,4},{4,6},{6,0},{1,3},{3,5},{5,7},{7,1},{8,10},{10,12},{12... | collective-permute-start | bytes 1376264 | tf_op jit(solution)/shard_map/ppermute | solution.py:221
  44.9 29.9 %all-to-all-start = ((bf16[32,56,128]{2,1,0:T(8,128)(2,1)}), bf16[32,56,128]{2,1,0:T(8,128)(2,1)S(1)}, u32[]{:S(2)}, u32[]{:S(2)}) async-start(bf16[32,56,128]{2,1,0:T(8,128)(2,1)} %bitcast_bitcast_fusion), calls=%async_computation | async-start | bytes 917504 | tf_op jit(solution)/shard_map/all_to_all | solution.py:225
  49.9 12.1 %collective-permute-start.9 = (bf16[16,112,128]{2,1,0:T(8,128)(2,1)S(1)}, bf16[16,112,128]{2,1,0:T(8,128)(2,1)S(1)}, u32[]{:S(2)}, u32[]{:S(2)}) collective-permute-start(bf16[16,112,128]{2,1,0:T(8,128)(2,1)S(1)} %bitcast.29), channel_id=1, source_target_pairs={{0,1},{1,0},{2,3},{3,2},{4,5},{5,4},{6,7},{7,6},{8,9},{9,8},{10,11... | collective-permute-start | bytes 1376264 | tf_op jit(solution)/shard_map/ppermute | solution.py:216
  50.6 12.2 %collective-permute-start.1 = (bf16[16,112,128]{2,1,0:T(8,128)(2,1)S(1)}, bf16[16,112,128]{2,1,0:T(8,128)(2,1)}, u32[]{:S(2)}, u32[]{:S(2)}) collective-permute-start(bf16[16,112,128]{2,1,0:T(8,128)(2,1)S(1)} %bitcast.30), channel_id=1, source_target_pairs={{0,6},{2,0},{4,2},{6,4},{1,7},{3,1},{5,3},{7,5},{8,14},{10,8},{12,... | collective-permute-start | bytes 1376264 | tf_op jit(solution)/shard_map/ppermute | solution.py:221
  52.1 20.5 %collective-permute-start = (bf16[16,112,128]{2,1,0:T(8,128)(2,1)S(1)}, bf16[16,112,128]{2,1,0:T(8,128)(2,1)}, u32[]{:S(2)}, u32[]{:S(2)}) collective-permute-start(bf16[16,112,128]{2,1,0:T(8,128)(2,1)S(1)} %bitcast.34), channel_id=1, source_target_pairs={{0,6},{2,0},{4,2},{6,4},{1,7},{3,1},{5,3},{7,5},{8,14},{10,8},{12,... | collective-permute-start | bytes 1376264 | tf_op jit(solution)/shard_map/ppermute | solution.py:221
  58.3 15.7 %collective-permute-start.10 = (bf16[16,112,128]{2,1,0:T(8,128)(2,1)S(1)}, bf16[16,112,128]{2,1,0:T(8,128)(2,1)S(1)}, u32[]{:S(2)}, u32[]{:S(2)}) collective-permute-start(bf16[16,112,128]{2,1,0:T(8,128)(2,1)S(1)} %collective-permute-done.4.refs_2_), channel_id=1, source_target_pairs={{0,1},{1,0},{2,3},{3,2},{4,5},{5,4},{6,7},{7,6},{8,9},{9,8},{10,11... | collective-permute-start | bytes 1376264 | tf_op jit(solution)/shard_map/ppermute | solution.py:216
  62.0 12.8 %collective-permute-start.11 = (bf16[16,112,128]{2,1,0:T(8,128)(2,1)S(1)}, bf16[16,112,128]{2,1,0:T(8,128)(2,1)}, u32[]{:S(2)}, u32[]{:S(2)}) collective-permute-start(bf16[16,112,128]{2,1,0:T(8,128)(2,1)S(1)} %collective-permute-done.7.refs_3_), channel_id=1, source_target_pairs={{0,1},{1,0},{2,3},{3,2},{4,5},{5,4},{6,7},{7,6},{8,9},{9,8},{10,11... | collective-permute-start | bytes 1376264 | tf_op jit(solution)/shard_map/ppermute | solution.py:216
  62.0 0.8 copy-start.1
  62.8 24.8 %collective-permute-start.5 = (bf16[16,112,128]{2,1,0:T(8,128)(2,1)S(1)}, bf16[16,112,128]{2,1,0:T(8,128)(2,1)}, u32[]{:S(2)}, u32[]{:S(2)}) collective-permute-start(bf16[16,112,128]{2,1,0:T(8,128)(2,1)S(1)} %collective-permute-done.4.refs_2_), channel_id=1, source_target_pairs={{0,2},{2,4},{4,6},{6,0},{1,3},{3,5},{5,7},{7,1},{8,10},{10,12},{12... | collective-permute-start | bytes 1376264 | tf_op jit(solution)/shard_map/ppermute | solution.py:221
  62.8 24.8 %collective-permute-start.6 = (bf16[16,112,128]{2,1,0:T(8,128)(2,1)}, bf16[16,112,128]{2,1,0:T(8,128)(2,1)}, u32[]{:S(2)}, u32[]{:S(2)}) collective-permute-start(bf16[16,112,128]{2,1,0:T(8,128)(2,1)} %collective-permute-done.1.refs_1_), channel_id=1, source_target_pairs={{0,6},{2,0},{4,2},{6,4},{1,7},{3,1},{5,3},{7,5},{8,14},{10,8},{12,... | collective-permute-start | bytes 1376264 | tf_op jit(solution)/shard_map/ppermute | solution.py:221
  72.5 16.0 %collective-permute-start.3 = (bf16[16,112,128]{2,1,0:T(8,128)(2,1)}, bf16[16,112,128]{2,1,0:T(8,128)(2,1)}, u32[]{:S(2)}, u32[]{:S(2)}) collective-permute-start(bf16[16,112,128]{2,1,0:T(8,128)(2,1)} %collective-permute-done.1.refs_1_), channel_id=1, source_target_pairs={{0,1},{1,0},{2,3},{3,2},{4,5},{5,4},{6,7},{7,6},{8,9},{9,8},{10,11... | collective-permute-start | bytes 1376264 | tf_op jit(solution)/shard_map/ppermute | solution.py:216
  74.0 0.8 copy-start.3
  74.8 13.7 %collective-permute-start.2 = (bf16[16,112,128]{2,1,0:T(8,128)(2,1)}, bf16[16,112,128]{2,1,0:T(8,128)(2,1)}, u32[]{:S(2)}, u32[]{:S(2)}) collective-permute-start(bf16[16,112,128]{2,1,0:T(8,128)(2,1)} %collective-permute-done.refs_0_), channel_id=1, source_target_pairs={{0,1},{1,0},{2,3},{3,2},{4,5},{5,4},{6,7},{7,6},{8,9},{9,8},{10,11... | collective-permute-start | bytes 1376264 | tf_op jit(solution)/shard_map/ppermute | solution.py:216
  74.8 1.0 copy-start.2
  75.8 1.0 copy-start.4
  87.6 2.4 %collective-permute-start.12 = (bf16[16,112,128]{2,1,0:T(8,128)(2,1)}, bf16[16,112,128]{2,1,0:T(8,128)(2,1)S(1)}, u32[]{:S(2)}, u32[]{:S(2)}) collective-permute-start(bf16[16,112,128]{2,1,0:T(8,128)(2,1)} %collective-permute-done.5.refs_4_), channel_id=1, source_target_pairs={{0,1},{1,0},{2,3},{3,2},{4,5},{5,4},{6,7},{7,6},{8,9},{9,8},{10,11... | collective-permute-start | bytes 1376264 | tf_op jit(solution)/shard_map/ppermute | solution.py:216
  88.4 2.3 %collective-permute-start.13 = (bf16[16,112,128]{2,1,0:T(8,128)(2,1)}, bf16[16,112,128]{2,1,0:T(8,128)(2,1)S(1)}, u32[]{:S(2)}, u32[]{:S(2)}) collective-permute-start(bf16[16,112,128]{2,1,0:T(8,128)(2,1)} %collective-permute-done.6.refs_5_), channel_id=1, source_target_pairs={{0,1},{1,0},{2,3},{3,2},{4,5},{5,4},{6,7},{7,6},{8,9},{9,8},{10,11... | collective-permute-start | bytes 1376264 | tf_op jit(solution)/shard_map/ppermute | solution.py:216
